TPU v7x, 32 devices: a whole 2x2x4 slice. The times are simulated.
32 devices in a mesh: dp: 4 (over y, x), row: 2 (over core), col: 4 (over z).
Axes of the slice: x: 2, y: 2, z: 4, core: 2. Of those that a mesh axis runs over, the one named last changes fastest.
Arguments:
- tokens: bfloat16 [3840, 4096], P(('dp', 'col'), 'row'), may hold values from -6 to 6
- hidden_cot: bfloat16 [3840, 14336], P(('dp', 'row'), 'col'), may hold values from -0.09667969 to 0.09667969
- gate_pre: bfloat16 [3840, 14336], P(('dp', 'row'), 'col'), may hold values from -10 to 10
- up_pre: bfloat16 [3840, 14336], P(('dp', 'row'), 'col'), may hold values from -6 to 6
Outputs:
- grad_gate: bfloat16 [2, 2048, 14336], P('row', 'dp', 'col')
All inputs are finite; a program needn't handle non-finite values.
Results may differ from a plain program's by a relative error of at most 0.014.
Values may be sent and summed in bfloat16 or wider, within the bound.
A program may use at most 128 MiB of HBM per device.

v0:
```python
import functools
import math

import jax
import jax.numpy as jnp
from jax import lax
from jax.experimental import pallas as pl
from jax.experimental.pallas import tpu as pltpu
from jax.sharding import PartitionSpec as P

MESH = pl.DeviceIdType.MESH


def near_square(n):
    nx = math.isqrt(n)
    while n % nx:
        nx -= 1
    return n // nx, nx


def kernel(dims, plan, tok, cot, gate, up, out, ins, grads, toks, tokt, part, got, res,
           in_sem, own_sem, ty_s, ty_r, tz_s, tz_r, gy_s, gy_r, gp_s, gp_r, x_s, x_r, out_sem):
    ny, nx, nr, nz, wide, block, chunks, cols = dims
    ahead, own_at = plan
    dp, r, z = lax.axis_index("dp"), lax.axis_index("row"), lax.axis_index("col")
    y, x = dp // nx, dp % nx
    subs = wide // block
    away = (nx - 1) * subs
    blocks = nx * subs
    rows = ny * nr * grads.shape[3]

    def at(oy=0, ox=0, orow=0, oz=0):
        return {
            "dp": (y + oy) % ny * nx + (x + ox) % nx,
            "row": (r + orow) % nr,
            "col": (z + oz) % nz,
        }

    def remote(src, dst, ss, rs, to):
        return pltpu.make_async_remote_copy(
            src_ref=src, dst_ref=dst, send_sem=ss, recv_sem=rs, device_id=to, device_id_type=MESH)

    def each(n, f):
        def body(i, c):
            f(i)
            return c
        lax.fori_loop(0, n, body, 0)

    def load(k, i):
        src = (cot, gate, up)[i]
        return pltpu.make_async_copy(
            src.at[:, pl.ds(pl.multiple_of(k * cols, cols), cols)], ins.at[i, k], in_sem.at[i, k])

    def tok_cols(oy, b):
        o, sub = (b // subs + 1) % nx, b % subs
        first = ((y + oy) % ny * nx + (x + o) % nx) * wide + sub * block
        return tok.at[:, pl.ds(pl.multiple_of(first, block), block)]

    def own_tok(b):
        return pltpu.make_async_copy(tok_cols(0, b), toks.at[b, y, z], own_sem.at[b])

    def tok_y(oy, b):
        return remote(tok_cols(oy, b), toks.at[b, y, z], ty_s.at[oy - 1, b], ty_r.at[oy - 1, b], at(oy=oy))

    reach = min(2, nz - 1)
    hops = ([(d, 0) for d in range(1, reach + 1)] + [(1, d) for d in range(2, nz - 1)])

    def valid(way, far, back):
        left = z >= back if way > 0 else z + back < nz
        right = z + far < nz if way > 0 else z >= far
        return jnp.logical_and(left, right)

    def tok_z(b, oy, way, i):
        far, back = hops[i]
        zs = z - way * back
        ref = toks.at[b, (y - oy + ny) % ny, zs]
        w = 0 if way > 0 else 1
        return remote(ref, ref, tz_s.at[w, i, b, oy], tz_r.at[zs, b, oy], at(oz=way * far + nz))

    def send_z(b, oy, relay, act):
        for way in (1, -1):
            for i, (far, back) in enumerate(hops):
                if (back > 0) == relay:
                    pl.when(valid(way, far, back))(functools.partial(lambda w, n: act(tok_z(b, oy, w, n)), way, i))

    def got_z(b, oy, zs):
        ref = toks.at[b, (y - oy + ny) % ny, zs]
        return remote(ref, ref, tz_s.at[0, 0, b, oy], tz_r.at[zs, b, oy], at(oz=1))

    def relay_z(b):
        for oy in range(ny):
            for way in (1, -1):
                for i, (far, back) in enumerate(hops):
                    if back:
                        def go(way=way, i=i, back=back, oy=oy):
                            got_z(b, oy, z - way * back).wait_recv()
                            tok_z(b, oy, way, i).start()
                        pl.when(valid(way, far, back))(go)

    def all_z(b):
        for oy in range(ny):
            for zs in range(nz):
                seen = jnp.bool_(False)
                for way in (1, -1):
                    for far, back in hops:
                        if back:
                            seen = jnp.logical_or(seen, jnp.logical_and(valid(way, far, back), z - way * back == zs))
                pl.when(jnp.logical_and(z != zs, jnp.logical_not(seen)))(got_z(b, oy, zs).wait_recv)

    def grad_y(oy, k):
        ref = grads.at[k, y, r]
        return remote(ref, ref, gy_s.at[oy - 1, k], gy_r.at[oy - 1, k], at(oy=oy))

    def grad_p(orow, oy, k):
        ref = grads.at[k, (y - oy + ny) % ny, r]
        return remote(ref, ref, gp_s.at[orow - 1, oy, k], gp_r.at[orow - 1, oy, k], at(orow=orow))

    def sum_x(b, k):
        return remote(part.at[b, k], got.at[b, k], x_s.at[b, k], x_r.at[b, k], at(ox=b // subs + 1))

    def write(sub, k):
        return pltpu.make_async_copy(
            res.at[sub, k],
            out.at[0, pl.ds(sub * block, block), pl.ds(pl.multiple_of(k * cols, cols), cols)],
            out_sem.at[sub, k])

    for b in range(blocks):
        own_tok(b).start()

    def load_all(k):
        for i in range(3):
            load(k, i).start()
    each(chunks, load_all)

    peers = ([at(oy=o) for o in range(1, ny)] + [at(ox=o) for o in range(1, nx)]
             + [at(orow=o) for o in range(1, nr)] + [at(oz=o) for o in range(1, nz)])
    barrier = pltpu.get_barrier_semaphore()
    for to in peers:
        pl.semaphore_signal(barrier, inc=1, device_id=to, device_id_type=MESH)
    pl.semaphore_wait(barrier, len(peers))

    def tok_out(b):
        for oy in range(1, ny):
            tok_y(oy, b).start()

    def own_out(b):
        own_tok(b).wait()
        send_z(b, 0, False, lambda c: c.start())

    def pass_on(b):
        for oy in range(1, ny):
            tok_y(oy, b).wait_recv()
            send_z(b, oy, False, lambda c: c.start())

    def gate_grad(k):
        for i in range(3):
            load(k, i).wait()
        step = 32
        tall = ins.shape[2]

        def rows_of(j, c):
            at_rows = pl.ds(pl.multiple_of(j * step, step), step)
            h = ins[0, k, at_rows, :].astype(jnp.float32)
            g = ins[1, k, at_rows, :].astype(jnp.float32)
            u = ins[2, k, at_rows, :].astype(jnp.float32)
            s = jax.nn.sigmoid(g)
            grads[k, y, r, at_rows, :] = (h * u * s * (1.0 + g * (1.0 - s))).astype(grads.dtype)
            return c
        lax.fori_loop(0, tall // step, rows_of, 0)
        for oy in range(1, ny):
            grad_y(oy, k).start()
        for orow in range(1, nr):
            grad_p(orow, 0, k).start()

    def feed(k):
        gate_grad(k)
        pl.when(k + lead < blocks)(lambda: tok_out(k + lead))

    def take_block(b):
        all_z(b)
        first = pl.multiple_of(b * block, block)
        tokt[pl.ds(first, block), :] = toks[b].reshape(rows, block).T

    def tile(b, k):
        left = tokt[pl.ds(pl.multiple_of(b * block, block), block), :]
        right = grads[k].reshape(rows, cols)
        part[b, k] = jnp.dot(left, right, preferred_element_type=jnp.float32).astype(part.dtype)
        sum_x(b, k).start()

    def finish(k):
        left = tokt[away * block:, :]
        total = jnp.dot(left, grads[k].reshape(rows, cols), preferred_element_type=jnp.float32)
        for sub in range(subs):
            sums = total[sub * block:(sub + 1) * block]
            for o in range(1, nx):
                b = (o - 1) * subs + sub
                sum_x(b, k).wait_recv()
                sums = sums + got[b, k].astype(jnp.float32)
            res[sub, k] = sums.astype(res.dtype)
            write(sub, k).start()

    def span(low, high, f):
        def body(i, c):
            f(i)
            return c
        lax.fori_loop(low, high, body, 0)

    def z_out(b):
        own_out(b)
        pass_on(b)

    def z_step(j):
        relay_z(j)
        pl.when(j + lead < blocks)(lambda: z_out(j + lead))

    relayed = lambda k: jnp.where(k >= own_at, blocks, jnp.minimum((2 * k + 5) * blocks // 24, blocks))
    ready = lambda k: jnp.where(k >= own_at, away, jnp.minimum((2 * k + 3) * away // 12, away))
    ended = lambda k: jnp.clip((k - own_at + 1) * 3, 0, chunks - 3)

    lead = min(2, blocks)
    for b in range(lead):
        tok_out(b)
    for b in range(lead):
        own_out(b)
    for b in range(lead):
        feed(b)
        pass_on(b)
    span(lead, ahead, feed)

    def main(k, c):
        pl.when(k + ahead < chunks)(lambda: feed(k + ahead))
        span(jnp.where(k > 0, relayed(k - 1), 0), relayed(k), z_step)
        for oy in range(1, ny):
            grad_y(oy, k).wait_recv()
            for orow in range(1, nr):
                grad_p(orow, oy, k).start()

        def catch_up(b):
            take_block(b)
            span(0, k, functools.partial(tile, b))
        now = ready(k)
        span(jnp.where(k > 0, ready(k - 1), 0), now, catch_up)

        @pl.when(k == own_at)
        def _():
            span(away, blocks, take_block)
        span(ended(k - 1), ended(k), finish)
        for orow in range(1, nr):
            for oy in range(ny):
                grad_p(orow, oy, k).wait_recv()
        span(0, now, lambda b: tile(b, k))
        return c
    lax.fori_loop(0, chunks, main, 0)
    span(ended(chunks - 1), chunks, finish)

    def done(b):
        for oy in range(1, ny):
            tok_y(oy, b).wait_send()
        for oy in range(ny):
            for relay in (False, True):
                send_z(b, oy, relay, lambda c: c.wait_send())
    each(blocks, done)

    def drain(k):
        for oy in range(1, ny):
            grad_y(oy, k).wait_send()
        for orow in range(1, nr):
            for oy in range(ny):
                grad_p(orow, oy, k).wait_send()
        for b in range(away):
            sum_x(b, k).wait_send()
        for sub in range(subs):
            write(sub, k).wait()
    each(chunks, drain)


def solution(mesh):
    ndp, nr, nz = mesh.shape["dp"], mesh.shape["row"], mesh.shape["col"]
    ny, nx = near_square(ndp)

    def on_device(tokens, hidden_cot, gate_pre, up_pre):
        tok_rows, wid = tokens.shape
        tall, hidden = gate_pre.shape
        wide = wid // ndp
        block = math.gcd(wide, 128)
        cols = math.gcd(hidden, 256)
        chunks = hidden // cols
        subs = wide // block
        blocks, away = nx * subs, (nx - 1) * subs
        rows = ny * nz * tok_rows
        dims = (ny, nx, nr, nz, wide, block, chunks, cols)
        plan = (min(8, chunks), max(chunks - 5, 0))
        dma = pltpu.SemaphoreType.DMA
        dt = tokens.dtype
        return pl.pallas_call(
            functools.partial(kernel, dims, plan),
            out_shape=jax.ShapeDtypeStruct((1, wide, hidden), dt),
            in_specs=[pl.BlockSpec(memory_space=pl.ANY)] * 4,
            out_specs=pl.BlockSpec(memory_space=pl.ANY),
            scratch_shapes=[
                pltpu.VMEM((3, chunks, tall, cols), dt),
                pltpu.VMEM((chunks, ny, nr, tall, cols), dt),
                pltpu.VMEM((blocks, ny, nz, tok_rows, block), dt),
                pltpu.VMEM((blocks * block, rows), dt),
                pltpu.VMEM((max(away, 1), chunks, block, cols), dt),
                pltpu.VMEM((max(away, 1), chunks, block, cols), dt),
                pltpu.VMEM((subs, chunks, block, cols), dt),
                dma((3, chunks)),
                dma((blocks,)),
                dma((max(ny - 1, 1), blocks)),
                dma((max(ny - 1, 1), blocks)),
                dma((2, max(2 * nz, 1), blocks, ny)),
                dma((nz, blocks, ny)),
                dma((max(ny - 1, 1), chunks)),
                dma((max(ny - 1, 1), chunks)),
                dma((max(nr - 1, 1), ny, chunks)),
                dma((max(nr - 1, 1), ny, chunks)),
                dma((max(away, 1), chunks)),
                dma((max(away, 1), chunks)),
                dma((subs, chunks)),
            ],
            compiler_params=pltpu.CompilerParams(
                collective_id=0, has_side_effects=True, vmem_limit_bytes=63 * 1024 * 1024
            ),
        )(tokens, hidden_cot, gate_pre, up_pre)

    in_specs = (
        P(("dp", "col"), "row"),
        P(("dp", "row"), "col"),
        P(("dp", "row"), "col"),
        P(("dp", "row"), "col"),
    )
    return jax.shard_map(
        on_device, mesh=mesh, in_specs=in_specs, out_specs=P("row", "dp", "col"), check_vma=False
    )
```

profile of v0, /device:TPU:0, one launch (start us, length us, event | category | flops | bytes accessed | tf_op | source)
XLA Modules:
  0.0 119.4 jit_solution(9104257669989552977)
XLA Ops:
  0.0 115.3 %shard_map.46 = bf16[1,512,3584]{2,1,0:T(8,128)(2,1)} custom-call(bf16[240,2048]{1,0:T(8,128)(2,1)} %tok.1, bf16[480,3584]{1,0:T(8,128)(2,1)} %cot.1, bf16[480,3584]{1,0:T(8,128)(2,1)} %gate.1, bf16[480,3584]{1,0:T(8,128)(2,1)} %up.1), custom_call_target="tpu_custom_call" | custom-call | tf_op jit(solution)/shard_map/pallas_call | solution.py:295
  115.3 4.1 %copy.6 = bf16[1,512,3584]{2,1,0:T(8,128)(2,1)} copy(bf16[1,512,3584]{2,1,0:T(8,128)(2,1)} %shard_map.46) | data formatting | bytes 7340032
where the time goes:
time: 120 us; the launch traced here: 119 us
  Pallas kernels  115 us (96%)
  local copies, waits for them, and re-layouts  4.11 us (3%)
    pallas_call x1, Pallas kernels, on_device(): pl.pallas_call(functools.partial(kernel, dims, plan), out_shape=jax.Shape...  115 us
    unnamed x1, local copies, waits for them, and re-layouts  4.11 us

commit v1 on v0

v1 whole, which is shorter than its diff:
```python
import functools
import math

import jax
import jax.numpy as jnp
from jax import lax
from jax.experimental import pallas as pl
from jax.experimental.pallas import tpu as pltpu
from jax.sharding import PartitionSpec as P

MESH = pl.DeviceIdType.MESH


def near_square(n):
    nx = math.isqrt(n)
    while n % nx:
        nx -= 1
    return n // nx, nx


def kernel(dims, plan, tok, cot, gate, up, out, ins, grads, toks, tokt, part, got,
           in_sem, own_sem, ty_s, ty_r, tz_s, tz_r, gy_s, gy_r, gp_s, gp_r, x_s, x_r):
    ny, nx, nr, nz, wide, block, chunks, cols = dims
    lead, ahead, own_at, per = plan
    dp, r, z = lax.axis_index("dp"), lax.axis_index("row"), lax.axis_index("col")
    y, x = dp // nx, dp % nx
    subs = wide // block
    away = (nx - 1) * subs
    blocks = nx * subs
    rows = ny * nr * grads.shape[3]

    def at(oy=0, ox=0, orow=0, oz=0):
        return {
            "dp": (y + oy) % ny * nx + (x + ox) % nx,
            "row": (r + orow) % nr,
            "col": (z + oz) % nz,
        }

    def remote(src, dst, ss, rs, to):
        return pltpu.make_async_remote_copy(
            src_ref=src, dst_ref=dst, send_sem=ss, recv_sem=rs, device_id=to, device_id_type=MESH)

    def span(low, high, f):
        def body(i, c):
            f(i)
            return c
        lax.fori_loop(low, high, body, 0)

    def load(k, i):
        src = (cot, gate, up)[i]
        return pltpu.make_async_copy(
            src.at[:, pl.ds(pl.multiple_of(k * cols, cols), cols)],
            ins.at[k, :, pl.ds(i * cols, cols)], in_sem.at[k])

    def loaded(k):
        pltpu.make_async_copy(cot.at[:, pl.ds(0, 3 * cols)], ins.at[k], in_sem.at[k]).wait()

    def tok_cols(oy, b):
        o, sub = (b // subs + 1) % nx, b % subs
        first = ((y + oy) % ny * nx + (x + o) % nx) * wide + sub * block
        return tok.at[:, pl.ds(pl.multiple_of(first, block), block)]

    def own_tok(b):
        return pltpu.make_async_copy(tok_cols(0, b), toks.at[b, y, z], own_sem.at[b])

    def tok_y(oy, b):
        return remote(tok_cols(oy, b), toks.at[b, y, z], ty_s.at[oy - 1], ty_r.at[oy - 1, b], at(oy=oy))

    reach = min(2, nz - 1)
    hops = ([(d, 0) for d in range(reach, 0, -1)] + [(1, d) for d in range(2, nz - 1)])
    relays = max(nz - 3, 0)

    def valid(way, far, back):
        left = z >= back if way > 0 else z + back < nz
        right = z + far < nz if way > 0 else z >= far
        return jnp.logical_and(left, right)

    def relay_sem(w, back, b, oy):
        return blocks + ((w * relays + back - 2) * blocks + b) * ny + oy

    def tok_z(b, oy, way, i):
        far, back = hops[i]
        ref = toks.at[b, (y - oy + ny) % ny, z - way * back]
        w, dist = (0 if way > 0 else 1), far + back
        sem = b
        if 2 <= dist <= nz - 2:
            beyond = z + way * (far + 1)
            goes_on = beyond < nz if way > 0 else beyond >= 0
            sem = jnp.where(goes_on, relay_sem(w, dist, b, oy), b)
        return remote(ref, ref, tz_s.at[w], tz_r.at[sem], at(oz=way * far + nz))

    def each_hop(relay, act):
        for i, (far, back) in enumerate(hops):
            if (back > 0) == relay:
                for way in (1, -1):
                    pl.when(valid(way, far, back))(functools.partial(act, way, i))

    def send_z(b, oy):
        each_hop(False, lambda way, i: tok_z(b, oy, way, i).start())

    def relay_z(b):
        for oy in range(ny):
            def go(way, i, oy=oy):
                back = hops[i][1]
                ref = toks.at[b, (y - oy + ny) % ny, z - way * back]
                w = 0 if way > 0 else 1
                remote(ref, ref, tz_s.at[w], tz_r.at[relay_sem(w, back, b, oy)], at(oz=1)).wait_recv()
                tok_z(b, oy, way, i).start()
            each_hop(True, go)

    def all_z(b):
        count = nz - 1
        for way in (1, -1):
            for far, back in hops:
                if back:
                    count = count - valid(way, far, back).astype(jnp.int32)
        for n in range(1, nz):
            ref = toks.at[b, :, pl.ds(0, n)]
            pl.when(count == n)(remote(ref, ref, tz_s.at[0], tz_r.at[b], at(oz=1)).wait_recv)

    def sent_z():
        for way in (1, -1):
            w = 0 if way > 0 else 1
            count = jnp.int32(0)
            for far, back in hops:
                count = count + valid(way, far, back).astype(jnp.int32)
            for n in range(1, nz):
                ref = toks.at[:, :, pl.ds(0, n)]
                pl.when(count == n)(remote(ref, ref, tz_s.at[w], tz_r.at[0], at(oz=1)).wait_send)

    def grad_y(oy, k):
        ref = grads.at[k, y, r]
        return remote(ref, ref, gy_s.at[oy - 1], gy_r.at[oy - 1, k], at(oy=oy))

    def grad_p(orow, oy, k):
        ref = grads.at[k, (y - oy + ny) % ny, r]
        return remote(ref, ref, gp_s.at[orow - 1], gp_r.at[orow - 1, k], at(orow=orow))

    def got_p(orow, k):
        ref = grads.at[k, :, (r - orow + nr) % nr]
        remote(ref, ref, gp_s.at[orow - 1], gp_r.at[orow - 1, k], at(orow=orow)).wait_recv()

    def sum_x(b, k):
        at_rows = pl.ds(pl.multiple_of(b * block, block), block)
        return remote(part.at[k, at_rows], got.at[k, at_rows], x_s.at[0], x_r.at[k], at(ox=b // subs + 1))

    span(0, blocks, lambda b: own_tok(b).start())

    def load_all(k):
        for i in range(3):
            load(k, i).start()
    span(0, chunks, load_all)

    peers = ([at(oy=o) for o in range(1, ny)] + [at(ox=o) for o in range(1, nx)]
             + [at(orow=o) for o in range(1, nr)] + [at(oz=o) for o in range(1, nz)])
    barrier = pltpu.get_barrier_semaphore()
    for to in peers:
        pl.semaphore_signal(barrier, inc=1, device_id=to, device_id_type=MESH)
    pl.semaphore_wait(barrier, len(peers))

    def tok_out(b):
        for oy in range(1, ny):
            tok_y(oy, b).start()

    def own_out(b):
        own_tok(b).wait()
        send_z(b, 0)

    def pass_on(b):
        for oy in range(1, ny):
            tok_y(oy, b).wait_recv()
            send_z(b, oy)

    def gate_grad(k):
        loaded(k)
        step = 32
        tall = ins.shape[1]

        def rows_of(j, c):
            at_rows = pl.ds(pl.multiple_of(j * step, step), step)
            h = ins[k, at_rows, 0:cols].astype(jnp.float32)
            g = ins[k, at_rows, cols:2 * cols].astype(jnp.float32)
            u = ins[k, at_rows, 2 * cols:3 * cols].astype(jnp.float32)
            s = jax.nn.sigmoid(g)
            grads[k, y, r, at_rows, :] = (h * u * s * (1.0 + g * (1.0 - s))).astype(grads.dtype)
            return c
        lax.fori_loop(0, tall // step, rows_of, 0)
        for oy in range(1, ny):
            grad_y(oy, k).start()
        for orow in range(1, nr):
            grad_p(orow, 0, k).start()

    def feed(k):
        gate_grad(k)
        pl.when(k + 1 < blocks)(lambda: tok_out(k + 1))

    def take_block(b):
        all_z(b)
        first = pl.multiple_of(b * block, block)
        tokt[pl.ds(first, block), :] = toks[b].reshape(rows, block).T

    def tile(b, k):
        at_rows = pl.ds(pl.multiple_of(b * block, block), block)
        right = grads[k].reshape(rows, cols)
        sums = jnp.dot(tokt[at_rows, :], right, preferred_element_type=jnp.float32)
        part[k, at_rows, :] = sums.astype(part.dtype)
        sum_x(b, k).start()

    def finish(k):
        left = tokt[away * block:, :]
        sums = jnp.dot(left, grads[k].reshape(rows, cols), preferred_element_type=jnp.float32)
        remote(got.at[k], got.at[k], x_s.at[0], x_r.at[k], at(ox=1)).wait_recv()
        for o in range(nx - 1):
            sums = sums + got[k, o * wide:(o + 1) * wide, :].astype(jnp.float32)
        out[0, :, pl.ds(pl.multiple_of(k * cols, cols), cols)] = sums.astype(out.dtype)

    def catch_up(k, b):
        take_block(b)
        span(0, k, functools.partial(tile, b))

    def pass_step(j):
        pass_on(j)
        pl.when(j + 1 < blocks)(lambda: own_out(j + 1))

    passed = lambda k: jnp.minimum(k + 2, blocks)
    relayed = lambda k: jnp.clip(jnp.where(k < away, k + 1, away + (k - away) * 5 // 6), 0, blocks)
    ready = lambda k: jnp.clip(k, 1, away)
    ended = lambda k: jnp.clip((k - own_at + 1) * per, 0, jnp.maximum(k - 1, 0))

    tok_out(0)
    own_out(0)
    span(0, lead, feed)
    pass_step(0)
    span(lead, ahead, feed)

    def main(k, c):
        span(jnp.where(k > 0, ready(k - 1), 1), ready(k), functools.partial(catch_up, k))
        for oy in range(1, ny):
            grad_y(oy, k).wait_recv()
            for orow in range(1, nr):
                grad_p(orow, oy, k).start()
        span(jnp.where(k > 0, relayed(k - 1), 0), relayed(k), relay_z)
        span(passed(k - 1), passed(k), pass_step)
        pl.when(k + ahead < chunks)(lambda: feed(k + ahead))
        pl.when(k == 0)(lambda: take_block(0))
        for orow in range(1, nr):
            got_p(orow, k)
        span(0, ready(k), lambda b: tile(b, k))

        @pl.when(k == own_at)
        def _():
            span(away, blocks, take_block)
        span(ended(k - 1), ended(k), finish)
        return c
    lax.fori_loop(0, chunks, main, 0)
    span(ended(chunks - 1), chunks, finish)

    for oy in range(1, ny):
        ref = toks.at[:, y, z]
        remote(ref, ref, ty_s.at[oy - 1], ty_r.at[oy - 1, 0], at(oy=oy)).wait_send()
        ref = grads.at[:, y, r]
        remote(ref, ref, gy_s.at[oy - 1], gy_r.at[oy - 1, 0], at(oy=oy)).wait_send()
    for orow in range(1, nr):
        ref = grads.at[:, :, r]
        remote(ref, ref, gp_s.at[orow - 1], gp_r.at[orow - 1, 0], at(orow=orow)).wait_send()
    sent_z()
    remote(part, part, x_s.at[0], x_r.at[0], at(ox=1)).wait_send()


def solution(mesh):
    ndp, nr, nz = mesh.shape["dp"], mesh.shape["row"], mesh.shape["col"]
    ny, nx = near_square(ndp)

    def on_device(tokens, hidden_cot, gate_pre, up_pre):
        tok_rows, wid = tokens.shape
        tall, hidden = gate_pre.shape
        wide = wid // ndp
        block = math.gcd(wide, 128)
        cols = math.gcd(hidden, 256)
        chunks = hidden // cols
        subs = wide // block
        blocks, away = nx * subs, (nx - 1) * subs
        rows = ny * nz * tok_rows
        relays = 2 * max(nz - 3, 0) * blocks * ny
        dims = (ny, nx, nr, nz, wide, block, chunks, cols)
        plan = (3, min(5, chunks), max(chunks - 4, 0), 4)
        dma = pltpu.SemaphoreType.DMA
        dt = tokens.dtype
        return pl.pallas_call(
            functools.partial(kernel, dims, plan),
            out_shape=pltpu.VMEM((1, wide, hidden), dt),
            in_specs=[pl.BlockSpec(memory_space=pl.ANY)] * 4,
            out_specs=pl.BlockSpec(memory_space=pltpu.VMEM),
            scratch_shapes=[
                pltpu.VMEM((chunks, tall, 3 * cols), dt),
                pltpu.VMEM((chunks, ny, nr, tall, cols), dt),
                pltpu.VMEM((blocks, ny, nz, tok_rows, block), dt),
                pltpu.VMEM((blocks * block, rows), dt),
                pltpu.VMEM((chunks, away * block, cols), dt),
                pltpu.VMEM((chunks, away * block, cols), dt),
                dma((chunks,)),
                dma((blocks,)),
                dma((ny - 1,)),
                dma((ny - 1, blocks)),
                dma((2,)),
                dma((blocks + relays,)),
                dma((ny - 1,)),
                dma((ny - 1, chunks)),
                dma((nr - 1,)),
                dma((nr - 1, chunks)),
                dma((1,)),
                dma((chunks,)),
            ],
            compiler_params=pltpu.CompilerParams(
                collective_id=0, has_side_effects=True, vmem_limit_bytes=56 * 1024 * 1024
            ),
        )(tokens, hidden_cot, gate_pre, up_pre)

    in_specs = (
        P(("dp", "col"), "row"),
        P(("dp", "row"), "col"),
        P(("dp", "row"), "col"),
        P(("dp", "row"), "col"),
    )
    return jax.shard_map(
        on_device, mesh=mesh, in_specs=in_specs, out_specs=P("row", "dp", "col"), check_vma=False
    )
```

time: 120 us -> 110 us (0.917)
  Pallas kernels: 115 us -> 108 us
  local copies, waits for them, and re-layouts: 4.11 us -> 1.84 us
    pallas_call x1, Pallas kernels: 115 us -> 108 us  [on_device(): pl.pallas_call(functools.partial(kernel, dims, plan), out_shape=pltpu.VME...]
    unnamed x1, local copies, waits for them, and re-layouts: 4.11 us -> 1.84 us
where the time goes in v1:
time: 110 us
  Pallas kernels  108 us (98%)
  local copies, waits for them, and re-layouts  1.84 us (2%)
    pallas_call x1, Pallas kernels, on_device(): pl.pallas_call(functools.partial(kernel, dims, plan), out_shape=pltpu.VME...  108 us

profile of v1, /device:TPU:0, one launch (start us, length us, event | category | flops | bytes accessed | tf_op | source)
XLA Modules:
  0.0 109.9 jit_solution(1107877158071508663)
XLA Ops:
  0.0 108.1 %shard_map.46 = bf16[1,512,3584]{2,1,0:T(8,128)(2,1)S(1)} custom-call(bf16[240,2048]{1,0:T(8,128)(2,1)} %tok.1, bf16[480,3584]{1,0:T(8,128)(2,1)} %cot.1, bf16[480,3584]{1,0:T(8,128)(2,1)} %gate.1, bf16[480,3584]{1,0:T(8,128)(2,1)} %up.1), custom_call_target="tpu_custom_call" | custom-call | tf_op jit(solution)/shard_map/pallas_call | solution.py:289
  108.1 1.8 %copy.6 = bf16[1,512,3584]{2,1,0:T(8,128)(2,1)} copy(bf16[1,512,3584]{2,1,0:T(8,128)(2,1)S(1)} %shard_map.46) | data formatting | bytes 7340032

commit v2 on v1

--- a/solution.py
+++ b/solution.py
@@ -47,13 +47,12 @@
         lax.fori_loop(low, high, body, 0)
 
     def load(k, i):
-        src = (cot, gate, up)[i]
-        return pltpu.make_async_copy(
-            src.at[:, pl.ds(pl.multiple_of(k * cols, cols), cols)],
-            ins.at[k, :, pl.ds(i * cols, cols)], in_sem.at[k])
-
-    def loaded(k):
-        pltpu.make_async_copy(cot.at[:, pl.ds(0, 3 * cols)], ins.at[k], in_sem.at[k]).wait()
+        at_cols = pl.ds(0, cols) if k == 0 else pl.ds(cols, (chunks - 1) * cols)
+        return pltpu.make_async_copy((cot, gate, up)[i].at[:, at_cols], ins.at[i, :, at_cols], in_sem.at[i, k])
+
+    def loads(k, act):
+        for i in range(3):
+            act(load(k, i))
 
     def tok_cols(oy, b):
         o, sub = (b // subs + 1) % nx, b % subs
@@ -76,17 +75,20 @@
         return jnp.logical_and(left, right)
 
     def relay_sem(w, back, b, oy):
+        w = w if nz > 4 else 0
         return blocks + ((w * relays + back - 2) * blocks + b) * ny + oy
+
+    def goes_on(way, far, back):
+        if not 2 <= far + back <= nz - 2:
+            return jnp.bool_(False)
+        beyond = z + way * (far + 1)
+        return beyond < nz if way > 0 else beyond >= 0
 
     def tok_z(b, oy, way, i):
         far, back = hops[i]
         ref = toks.at[b, (y - oy + ny) % ny, z - way * back]
         w, dist = (0 if way > 0 else 1), far + back
-        sem = b
-        if 2 <= dist <= nz - 2:
-            beyond = z + way * (far + 1)
-            goes_on = beyond < nz if way > 0 else beyond >= 0
-            sem = jnp.where(goes_on, relay_sem(w, dist, b, oy), b)
+        sem = jnp.where(goes_on(way, far, back), relay_sem(w, dist, b, oy), b)
         return remote(ref, ref, tz_s.at[w], tz_r.at[sem], at(oz=way * far + nz))
 
     def each_hop(relay, act):
@@ -95,11 +97,20 @@
                 for way in (1, -1):
                     pl.when(valid(way, far, back))(functools.partial(act, way, i))
 
-    def send_z(b, oy):
-        each_hop(False, lambda way, i: tok_z(b, oy, way, i).start())
-
-    def relay_z(b):
-        for oy in range(ny):
+    def send_z(b, oy, part):
+        def go(way, i):
+            far, back = hops[i]
+            send = tok_z(b, oy, way, i).start
+            if part == "all":
+                send()
+            elif part == "far":
+                pl.when(goes_on(way, far, back))(send)
+            else:
+                pl.when(jnp.logical_not(goes_on(way, far, back)))(send)
+        each_hop(False, go)
+
+    def relay_z(group, b):
+        for oy in group:
             def go(way, i, oy=oy):
                 back = hops[i][1]
                 ref = toks.at[b, (y - oy + ny) % ny, z - way * back]
@@ -146,10 +157,8 @@
 
     span(0, blocks, lambda b: own_tok(b).start())
 
-    def load_all(k):
-        for i in range(3):
-            load(k, i).start()
-    span(0, chunks, load_all)
+    for k in range(2):
+        loads(k, lambda c: c.start())
 
     peers = ([at(oy=o) for o in range(1, ny)] + [at(ox=o) for o in range(1, nx)]
              + [at(orow=o) for o in range(1, nr)] + [at(oz=o) for o in range(1, nz)])
@@ -164,23 +173,25 @@
 
     def own_out(b):
         own_tok(b).wait()
-        send_z(b, 0)
+        send_z(b, 0, "far")
 
     def pass_on(b):
         for oy in range(1, ny):
             tok_y(oy, b).wait_recv()
-            send_z(b, oy)
+            send_z(b, oy, "all")
 
     def gate_grad(k):
-        loaded(k)
+        for g in range(2):
+            pl.when(k == g)(functools.partial(loads, g, lambda c: c.wait()))
         step = 32
         tall = ins.shape[1]
+        at_cols = pl.ds(pl.multiple_of(k * cols, cols), cols)
 
         def rows_of(j, c):
             at_rows = pl.ds(pl.multiple_of(j * step, step), step)
-            h = ins[k, at_rows, 0:cols].astype(jnp.float32)
-            g = ins[k, at_rows, cols:2 * cols].astype(jnp.float32)
-            u = ins[k, at_rows, 2 * cols:3 * cols].astype(jnp.float32)
+            h = ins[0, at_rows, at_cols].astype(jnp.float32)
+            g = ins[1, at_rows, at_cols].astype(jnp.float32)
+            u = ins[2, at_rows, at_cols].astype(jnp.float32)
             s = jax.nn.sigmoid(g)
             grads[k, y, r, at_rows, :] = (h * u * s * (1.0 + g * (1.0 - s))).astype(grads.dtype)
             return c
@@ -223,23 +234,34 @@
         pl.when(j + 1 < blocks)(lambda: own_out(j + 1))
 
     passed = lambda k: jnp.minimum(k + 2, blocks)
+    rest = lambda b: send_z(b, 0, "rest")
+    own_relay = functools.partial(relay_z, (0,))
+    got_relay = functools.partial(relay_z, range(1, ny))
+    early = lambda k: jnp.minimum(relayed(k) + 1, blocks)
     relayed = lambda k: jnp.clip(jnp.where(k < away, k + 1, away + (k - away) * 5 // 6), 0, blocks)
     ready = lambda k: jnp.clip(k, 1, away)
     ended = lambda k: jnp.clip((k - own_at + 1) * per, 0, jnp.maximum(k - 1, 0))
 
     tok_out(0)
     own_out(0)
+    rest(0)
     span(0, lead, feed)
     pass_step(0)
     span(lead, ahead, feed)
+    own_relay(0)
 
     def main(k, c):
-        span(jnp.where(k > 0, ready(k - 1), 1), ready(k), functools.partial(catch_up, k))
+        late = k == away
+        span(jnp.where(late, away, ready(k - 1)), ready(k), functools.partial(catch_up, k))
         for oy in range(1, ny):
             grad_y(oy, k).wait_recv()
             for orow in range(1, nr):
                 grad_p(orow, oy, k).start()
-        span(jnp.where(k > 0, relayed(k - 1), 0), relayed(k), relay_z)
+        before = jnp.where(k > 0, relayed(k - 1), 0)
+        span(before, relayed(k), got_relay)
+        span(jnp.where(late, ready(k - 1), away), away, functools.partial(catch_up, k))
+        span(passed(k - 1), passed(k), rest)
+        span(jnp.minimum(before + 1, blocks), early(k), own_relay)
         span(passed(k - 1), passed(k), pass_step)
         pl.when(k + ahead < chunks)(lambda: feed(k + ahead))
         pl.when(k == 0)(lambda: take_block(0))
@@ -281,7 +303,7 @@
         subs = wide // block
         blocks, away = nx * subs, (nx - 1) * subs
         rows = ny * nz * tok_rows
-        relays = 2 * max(nz - 3, 0) * blocks * ny
+        relays = (2 if nz > 4 else 1) * max(nz - 3, 0) * blocks * ny
         dims = (ny, nx, nr, nz, wide, block, chunks, cols)
         plan = (3, min(5, chunks), max(chunks - 4, 0), 4)
         dma = pltpu.SemaphoreType.DMA
@@ -292,13 +314,13 @@
             in_specs=[pl.BlockSpec(memory_space=pl.ANY)] * 4,
             out_specs=pl.BlockSpec(memory_space=pltpu.VMEM),
             scratch_shapes=[
-                pltpu.VMEM((chunks, tall, 3 * cols), dt),
+                pltpu.VMEM((3, tall, hidden), dt),
                 pltpu.VMEM((chunks, ny, nr, tall, cols), dt),
                 pltpu.VMEM((blocks, ny, nz, tok_rows, block), dt),
                 pltpu.VMEM((blocks * block, rows), dt),
                 pltpu.VMEM((chunks, away * block, cols), dt),
                 pltpu.VMEM((chunks, away * block, cols), dt),
-                dma((chunks,)),
+                dma((3, 2)),
                 dma((blocks,)),
                 dma((ny - 1,)),
                 dma((ny - 1, blocks)),

time: 110 us -> 109 us (level)
    pallas_call x1, Pallas kernels: 108 us -> 107 us  [on_device(): pl.pallas_call(functools.partial(kernel, dims, plan), out_shape=pltpu.VME...]
where the time goes in v2:
time: 109 us
  Pallas kernels  107 us (98%)
  local copies, waits for them, and re-layouts  1.84 us (2%)
    pallas_call x1, Pallas kernels, on_device(): pl.pallas_call(functools.partial(kernel, dims, plan), out_shape=pltpu.VME...  107 us

profile of v2, /device:TPU:0, one launch (start us, length us, event | category | flops | bytes accessed | tf_op | source)
XLA Modules:
  0.0 108.8 jit_solution(3288264407533553205)
XLA Ops:
  0.0 106.9 %shard_map.46 = bf16[1,512,3584]{2,1,0:T(8,128)(2,1)S(1)} custom-call(bf16[240,2048]{1,0:T(8,128)(2,1)} %tok.1, bf16[480,3584]{1,0:T(8,128)(2,1)} %cot.1, bf16[480,3584]{1,0:T(8,128)(2,1)} %gate.1, bf16[480,3584]{1,0:T(8,128)(2,1)} %up.1), custom_call_target="tpu_custom_call" | custom-call | tf_op jit(solution)/shard_map/pallas_call | solution.py:311
  106.9 1.8 %copy.6 = bf16[1,512,3584]{2,1,0:T(8,128)(2,1)} copy(bf16[1,512,3584]{2,1,0:T(8,128)(2,1)S(1)} %shard_map.46) | data formatting | bytes 7340032

commit v3 on v2

--- a/solution.py
+++ b/solution.py
@@ -19,14 +19,18 @@
 
 
 def kernel(dims, plan, tok, cot, gate, up, out, ins, grads, toks, tokt, part, got,
-           in_sem, own_sem, ty_s, ty_r, tz_s, tz_r, gy_s, gy_r, gp_s, gp_r, x_s, x_r):
+           gx, part2, own2, got2, in_sem, own_sem, ty_s, ty_r, tz_s, tz_r, gy_s, gy_r, gp_s, gp_r, x_s, x_r,
+           tx_s, tx_r, gx_s, gx_r, gq_s, gq_r, p2_s, p2_r):
     ny, nx, nr, nz, wide, block, chunks, cols = dims
-    lead, ahead, own_at, per = plan
+    lead, ahead, own_at, per, lite = plan
     dp, r, z = lax.axis_index("dp"), lax.axis_index("row"), lax.axis_index("col")
     y, x = dp // nx, dp % nx
     subs = wide // block
     away = (nx - 1) * subs
     blocks = nx * subs
+    plain = chunks - lite
+    every = blocks + (2 if lite else 0)
+    last = every - 1
     rows = ny * nr * grads.shape[3]
 
     def at(oy=0, ox=0, orow=0, oz=0):
@@ -59,6 +63,20 @@
         first = ((y + oy) % ny * nx + (x + o) % nx) * wide + sub * block
         return tok.at[:, pl.ds(pl.multiple_of(first, block), block)]
 
+    def tok_of(oy, ox, sub):
+        first = ((y + oy) % ny * nx + (x + ox) % nx) * wide + sub * block
+        return tok.at[:, pl.ds(pl.multiple_of(first, block), block)]
+
+    def tok_x(i):
+        dst = toks.at[blocks + i, x, z]
+        return remote(tok_of(1 - i, 1, subs - 1), dst, tx_s.at[0], tx_r.at[i], at(ox=1))
+
+    def own_more():
+        return pltpu.make_async_copy(tok_of(1, 0, subs - 1), toks.at[blocks, x, z], own_sem.at[blocks])
+
+    def source(b, oy):
+        return (jnp.where(b >= blocks, x, y) - oy + ny) % ny
+
     def own_tok(b):
         return pltpu.make_async_copy(tok_cols(0, b), toks.at[b, y, z], own_sem.at[b])
 
@@ -76,7 +94,7 @@
 
     def relay_sem(w, back, b, oy):
         w = w if nz > 4 else 0
-        return blocks + ((w * relays + back - 2) * blocks + b) * ny + oy
+        return every + ((w * relays + back - 2) * every + b) * ny + oy
 
     def goes_on(way, far, back):
         if not 2 <= far + back <= nz - 2:
@@ -86,24 +104,22 @@
 
     def tok_z(b, oy, way, i):
         far, back = hops[i]
-        ref = toks.at[b, (y - oy + ny) % ny, z - way * back]
+        ref = toks.at[b, source(b, oy), z - way * back]
         w, dist = (0 if way > 0 else 1), far + back
         sem = jnp.where(goes_on(way, far, back), relay_sem(w, dist, b, oy), b)
-        return remote(ref, ref, tz_s.at[w], tz_r.at[sem], at(oz=way * far + nz))
+        return remote(ref, ref, tz_s.at[w, jnp.where(b >= blocks + 1, 1, 0)], tz_r.at[sem], at(oz=way * far + nz))
 
     def each_hop(relay, act):
-        for i, (far, back) in enumerate(hops):
-            if (back > 0) == relay:
-                for way in (1, -1):
+        for way in (1, -1):
+            for i, (far, back) in sorted(enumerate(hops), key=lambda h: way * h[1][0]):
+                if (back > 0) == relay:
                     pl.when(valid(way, far, back))(functools.partial(act, way, i))
 
     def send_z(b, oy, part):
         def go(way, i):
             far, back = hops[i]
             send = tok_z(b, oy, way, i).start
-            if part == "all":
-                send()
-            elif part == "far":
+            if part == "far":
                 pl.when(goes_on(way, far, back))(send)
             else:
                 pl.when(jnp.logical_not(goes_on(way, far, back)))(send)
@@ -113,21 +129,21 @@
         for oy in group:
             def go(way, i, oy=oy):
                 back = hops[i][1]
-                ref = toks.at[b, (y - oy + ny) % ny, z - way * back]
+                ref = toks.at[b, source(b, oy), z - way * back]
                 w = 0 if way > 0 else 1
-                remote(ref, ref, tz_s.at[w], tz_r.at[relay_sem(w, back, b, oy)], at(oz=1)).wait_recv()
+                remote(ref, ref, tz_s.at[w, 0], tz_r.at[relay_sem(w, back, b, oy)], at(oz=1)).wait_recv()
                 tok_z(b, oy, way, i).start()
             each_hop(True, go)
 
-    def all_z(b):
+    def all_z(b, slots=ny):
         count = nz - 1
         for way in (1, -1):
             for far, back in hops:
                 if back:
                     count = count - valid(way, far, back).astype(jnp.int32)
         for n in range(1, nz):
-            ref = toks.at[b, :, pl.ds(0, n)]
-            pl.when(count == n)(remote(ref, ref, tz_s.at[0], tz_r.at[b], at(oz=1)).wait_recv)
+            ref = toks.at[b, pl.ds(0, slots), pl.ds(0, n)]
+            pl.when(count == n)(remote(ref, ref, tz_s.at[0, 0], tz_r.at[b], at(oz=1)).wait_recv)
 
     def sent_z():
         for way in (1, -1):
@@ -136,8 +152,12 @@
             for far, back in hops:
                 count = count + valid(way, far, back).astype(jnp.int32)
             for n in range(1, nz):
-                ref = toks.at[:, :, pl.ds(0, n)]
-                pl.when(count == n)(remote(ref, ref, tz_s.at[w], tz_r.at[0], at(oz=1)).wait_send)
+                most = blocks + 1 if lite else blocks
+                ref = toks.at[pl.ds(0, most), :, pl.ds(0, n)]
+                pl.when(count == n)(remote(ref, ref, tz_s.at[w, 0], tz_r.at[0], at(oz=1)).wait_send)
+                if lite:
+                    ref = toks.at[last, pl.ds(0, 1), pl.ds(0, n)]
+                    pl.when(count == n)(remote(ref, ref, tz_s.at[w, 1], tz_r.at[0], at(oz=1)).wait_send)
 
     def grad_y(oy, k):
         ref = grads.at[k, y, r]
@@ -153,32 +173,64 @@
 
     def sum_x(b, k):
         at_rows = pl.ds(pl.multiple_of(b * block, block), block)
-        return remote(part.at[k, at_rows], got.at[k, at_rows], x_s.at[0], x_r.at[k], at(ox=b // subs + 1))
+        sent = x_s.at[jnp.where(k >= plain, 1, 0)]
+        return remote(part.at[k, at_rows], got.at[k, at_rows], sent, x_r.at[k], at(ox=b // subs + 1))
+
+    def grad_x(i):
+        return remote(grads.at[plain + i, y, r], gx.at[i, x, r], gx_s.at[0], gx_r.at[i], at(ox=1))
+
+    def grad_q(i, ox):
+        dst = gx.at[i, (x + ox) % nx, r]
+        src = dst if ox else grads.at[plain + i, y, r]
+        return remote(src, dst, gq_s.at[0], gq_r.at[i], at(orow=1))
+
+    def got_q(i):
+        ref = gx.at[i, :, (r + 1) % nr]
+        remote(ref, ref, gq_s.at[0], gq_r.at[i], at(orow=1)).wait_recv()
+
+    def sum_y(i):
+        return remote(part2.at[i], got2.at[i], p2_s.at[0], p2_r.at[i], at(oy=1))
 
     span(0, blocks, lambda b: own_tok(b).start())
+    if lite:
+        own_more().start()
 
     for k in range(2):
         loads(k, lambda c: c.start())
 
     peers = ([at(oy=o) for o in range(1, ny)] + [at(ox=o) for o in range(1, nx)]
-             + [at(orow=o) for o in range(1, nr)] + [at(oz=o) for o in range(1, nz)])
+             + [at(orow=o) for o in range(1, nr)])
     barrier = pltpu.get_barrier_semaphore()
+
+    def greet(to):
+        pl.semaphore_signal(barrier, inc=1, device_id=to, device_id_type=MESH)
     for to in peers:
-        pl.semaphore_signal(barrier, inc=1, device_id=to, device_id_type=MESH)
-    pl.semaphore_wait(barrier, len(peers))
+        greet(to)
+    met = jnp.int32(len(peers))
+    for far in range(1, reach + 1):
+        for way in (1, -1):
+            there = valid(way, far, 0)
+            pl.when(there)(functools.partial(greet, at(oz=way * far + nz)))
+            met = met + there.astype(jnp.int32)
+    pl.semaphore_wait(barrier, met)
 
     def tok_out(b):
         for oy in range(1, ny):
             tok_y(oy, b).start()
 
     def own_out(b):
-        own_tok(b).wait()
+        pl.when(b < blocks)(lambda: own_tok(b).wait())
+        if lite:
+            pl.when(b == blocks)(lambda: own_more().wait())
         send_z(b, 0, "far")
 
     def pass_on(b):
         for oy in range(1, ny):
-            tok_y(oy, b).wait_recv()
-            send_z(b, oy, "all")
+            pl.when(b < blocks)(lambda: tok_y(oy, b).wait_recv())
+            if lite:
+                pl.when(b >= blocks)(lambda: tok_x(b - blocks).wait_recv())
+            send_z(b, oy, "far")
+            send_z(b, oy, "rest")
 
     def gate_grad(k):
         for g in range(2):
@@ -196,13 +248,13 @@
             grads[k, y, r, at_rows, :] = (h * u * s * (1.0 + g * (1.0 - s))).astype(grads.dtype)
             return c
         lax.fori_loop(0, tall // step, rows_of, 0)
+        for orow in range(1, nr):
+            grad_p(orow, 0, k).start()
+
+    def feed(k):
+        pl.when(k < plain)(lambda: gate_grad(k))
         for oy in range(1, ny):
             grad_y(oy, k).start()
-        for orow in range(1, nr):
-            grad_p(orow, 0, k).start()
-
-    def feed(k):
-        gate_grad(k)
         pl.when(k + 1 < blocks)(lambda: tok_out(k + 1))
 
     def take_block(b):
@@ -218,7 +270,7 @@
         sum_x(b, k).start()
 
     def finish(k):
-        left = tokt[away * block:, :]
+        left = tokt[away * block:blocks * block, :]
         sums = jnp.dot(left, grads[k].reshape(rows, cols), preferred_element_type=jnp.float32)
         remote(got.at[k], got.at[k], x_s.at[0], x_r.at[k], at(ox=1)).wait_recv()
         for o in range(nx - 1):
@@ -233,22 +285,72 @@
         pass_on(j)
         pl.when(j + 1 < blocks)(lambda: own_out(j + 1))
 
-    passed = lambda k: jnp.minimum(k + 2, blocks)
-    rest = lambda b: send_z(b, 0, "rest")
+    passed = lambda k: jnp.minimum(jnp.minimum(k + 2, blocks) + more(k, chunks - 5) + more(k, chunks - 4), every)
+    own_blocks = blocks + 1 if lite else blocks
+
+    def rest(b):
+        if lite:
+            pl.when(b == blocks)(lambda: own_out(b))
+        pl.when(b < own_blocks)(lambda: send_z(b, 0, "rest"))
+
     own_relay = functools.partial(relay_z, (0,))
     got_relay = functools.partial(relay_z, range(1, ny))
-    early = lambda k: jnp.minimum(relayed(k) + 1, blocks)
-    relayed = lambda k: jnp.clip(jnp.where(k < away, k + 1, away + (k - away) * 5 // 6), 0, blocks)
+    more = lambda k, at_step: jnp.where(k >= at_step, 1, 0)
+    early = lambda k: jnp.minimum(jnp.minimum(relayed(k) + 1, blocks) + more(k, chunks - 3), own_blocks)
+    relayed = lambda k: jnp.minimum(
+        jnp.clip(jnp.where(k < away, k + 1, away + (k - away) * 5 // 6), 0, blocks)
+        + more(k, chunks - 3) + more(k, chunks - 2), every)
     ready = lambda k: jnp.clip(k, 1, away)
-    ended = lambda k: jnp.clip((k - own_at + 1) * per, 0, jnp.maximum(k - 1, 0))
+    ended = lambda k: jnp.clip((k - own_at + 1) * per, 0, jnp.minimum(jnp.clip(k - 1, 0, plain), 2 * per))
 
     tok_out(0)
     own_out(0)
     rest(0)
+    if lite:
+        for i in range(2):
+            tok_x(i).start()
     span(0, lead, feed)
+
+    def over_x(i):
+        gate_grad(plain + i)
+        grad_x(i).start()
+        grad_q(i, 0).start()
+    if lite:
+        over_x(0)
     pass_step(0)
+    if lite:
+        span(1, lite, over_x)
     span(lead, ahead, feed)
     own_relay(0)
+
+    def over_y():
+        for i in range(lite):
+            grad_x(i).wait_recv()
+            grad_q(i, 1).start()
+        take_block(blocks)
+        all_z(last, 1)
+        toks[last, x] = toks[blocks - 1, y]
+        tokt[last * block:, :] = toks[last].reshape(rows, block).T
+
+        def sums(i):
+            got_q(i)
+            gx[i, x, r] = grads[plain + i, y, r]
+            both = jnp.dot(tokt[blocks * block:, :], gx[i].reshape(rows, cols), preferred_element_type=jnp.float32)
+            part2[i] = both[:block].astype(part2.dtype)
+            sum_y(i).start()
+            own2[i] = both[block:]
+        span(0, lite, sums)
+
+    def finish_last(i):
+        k, most = plain + i, (away - 1) * block
+        total = jnp.dot(tokt[away * block:away * block + most, :], grads[k].reshape(rows, cols),
+                        preferred_element_type=jnp.float32)
+        at_rows = pl.ds(0, most)
+        remote(got.at[k, at_rows], got.at[k, at_rows], x_s.at[1], x_r.at[k], at(ox=1)).wait_recv()
+        at_cols = pl.ds(pl.multiple_of(k * cols, cols), cols)
+        out[0, 0:most, at_cols] = (total + got[k, 0:most, :].astype(jnp.float32)).astype(out.dtype)
+        sum_y(i).wait_recv()
+        out[0, most:, at_cols] = (own2[i] + got2[i].astype(jnp.float32)).astype(out.dtype)
 
     def main(k, c):
         late = k == away
@@ -261,24 +363,28 @@
         span(before, relayed(k), got_relay)
         span(jnp.where(late, ready(k - 1), away), away, functools.partial(catch_up, k))
         span(passed(k - 1), passed(k), rest)
-        span(jnp.minimum(before + 1, blocks), early(k), own_relay)
+        span(early(k - 1), early(k), own_relay)
         span(passed(k - 1), passed(k), pass_step)
         pl.when(k + ahead < chunks)(lambda: feed(k + ahead))
         pl.when(k == 0)(lambda: take_block(0))
         for orow in range(1, nr):
             got_p(orow, k)
-        span(0, ready(k), lambda b: tile(b, k))
+        span(0, jnp.where(k >= plain, away - 1, ready(k)), lambda b: tile(b, k))
 
         @pl.when(k == own_at)
         def _():
             span(away, blocks, take_block)
+        if lite:
+            pl.when(k == chunks - 2)(over_y)
         span(ended(k - 1), ended(k), finish)
         return c
     lax.fori_loop(0, chunks, main, 0)
-    span(ended(chunks - 1), chunks, finish)
+    span(ended(chunks - 1), plain, finish)
+    if lite:
+        span(0, lite, finish_last)
 
     for oy in range(1, ny):
-        ref = toks.at[:, y, z]
+        ref = toks.at[pl.ds(0, blocks), y, z]
         remote(ref, ref, ty_s.at[oy - 1], ty_r.at[oy - 1, 0], at(oy=oy)).wait_send()
         ref = grads.at[:, y, r]
         remote(ref, ref, gy_s.at[oy - 1], gy_r.at[oy - 1, 0], at(oy=oy)).wait_send()
@@ -286,7 +392,18 @@
         ref = grads.at[:, :, r]
         remote(ref, ref, gp_s.at[orow - 1], gp_r.at[orow - 1, 0], at(orow=orow)).wait_send()
     sent_z()
-    remote(part, part, x_s.at[0], x_r.at[0], at(ox=1)).wait_send()
+    ref = part.at[pl.ds(0, plain)]
+    remote(ref, ref, x_s.at[0], x_r.at[0], at(ox=1)).wait_send()
+    if lite:
+        ref = part.at[pl.ds(plain, lite), pl.ds(0, (away - 1) * block)]
+        remote(ref, ref, x_s.at[1], x_r.at[0], at(ox=1)).wait_send()
+        ref = toks.at[pl.ds(blocks, 2), x, z]
+        remote(ref, ref, tx_s.at[0], tx_r.at[0], at(ox=1)).wait_send()
+        ref = grads.at[pl.ds(plain, lite), y, r]
+        remote(ref, ref, gx_s.at[0], gx_r.at[0], at(ox=1)).wait_send()
+        ref = gx.at[:, :, r]
+        remote(ref, ref, gq_s.at[0], gq_r.at[0], at(orow=1)).wait_send()
+        remote(part2, part2, p2_s.at[0], p2_r.at[0], at(oy=1)).wait_send()
 
 
 def solution(mesh):
@@ -303,9 +420,12 @@
         subs = wide // block
         blocks, away = nx * subs, (nx - 1) * subs
         rows = ny * nz * tok_rows
-        relays = (2 if nz > 4 else 1) * max(nz - 3, 0) * blocks * ny
+        lite = 3 if nx == ny == nr == 2 and subs > 1 and chunks > 10 else 0
+        every = blocks + (2 if lite else 0)
+        more = max(lite, 1)
+        relays = (2 if nz > 4 else 1) * max(nz - 3, 0) * every * ny
         dims = (ny, nx, nr, nz, wide, block, chunks, cols)
-        plan = (3, min(5, chunks), max(chunks - 4, 0), 4)
+        plan = (3, min(5, chunks), max(chunks - 4, 0), 3, lite)
         dma = pltpu.SemaphoreType.DMA
         dt = tokens.dtype
         return pl.pallas_call(
@@ -316,22 +436,34 @@
             scratch_shapes=[
                 pltpu.VMEM((3, tall, hidden), dt),
                 pltpu.VMEM((chunks, ny, nr, tall, cols), dt),
-                pltpu.VMEM((blocks, ny, nz, tok_rows, block), dt),
-                pltpu.VMEM((blocks * block, rows), dt),
+                pltpu.VMEM((every, ny, nz, tok_rows, block), dt),
+                pltpu.VMEM((every * block, rows), dt),
                 pltpu.VMEM((chunks, away * block, cols), dt),
                 pltpu.VMEM((chunks, away * block, cols), dt),
+                pltpu.VMEM((more, nx, nr, tall, cols), dt) if lite else pltpu.VMEM((1, 1, 1, 16, 128), dt),
+                pltpu.VMEM((more, block, cols), dt),
+                pltpu.VMEM((more, block, cols), jnp.float32),
+                pltpu.VMEM((more, block, cols), dt),
                 dma((3, 2)),
-                dma((blocks,)),
+                dma((every,)),
                 dma((ny - 1,)),
                 dma((ny - 1, blocks)),
-                dma((2,)),
-                dma((blocks + relays,)),
+                dma((2, 2)),
+                dma((every + relays,)),
                 dma((ny - 1,)),
                 dma((ny - 1, chunks)),
                 dma((nr - 1,)),
                 dma((nr - 1, chunks)),
+                dma((2,)),
+                dma((chunks,)),
                 dma((1,)),
-                dma((chunks,)),
+                dma((2,)),
+                dma((1,)),
+                dma((more,)),
+                dma((1,)),
+                dma((more,)),
+                dma((1,)),
+                dma((more,)),
             ],
             compiler_params=pltpu.CompilerParams(
                 collective_id=0, has_side_effects=True, vmem_limit_bytes=56 * 1024 * 1024

time: 109 us -> 104 us (0.954)
  Pallas kernels: 107 us -> 102 us
    pallas_call x1, Pallas kernels: 107 us -> 102 us  [on_device(): pl.pallas_call(functools.partial(kernel, dims, plan), out_shape=pltpu.VME...]
where the time goes in v3:
time: 104 us
  Pallas kernels  102 us (98%)
  local copies, waits for them, and re-layouts  1.84 us (2%)
    pallas_call x1, Pallas kernels, on_device(): pl.pallas_call(functools.partial(kernel, dims, plan), out_shape=pltpu.VME...  102 us

profile of v3, /device:TPU:0, one launch (start us, length us, event | category | flops | bytes accessed | tf_op | source)
XLA Modules:
  0.0 104.1 jit_solution(18095710151992018785)
XLA Ops:
  0.0 102.3 %shard_map.46 = bf16[1,512,3584]{2,1,0:T(8,128)(2,1)S(1)} custom-call(bf16[240,2048]{1,0:T(8,128)(2,1)} %tok.1, bf16[480,3584]{1,0:T(8,128)(2,1)} %cot.1, bf16[480,3584]{1,0:T(8,128)(2,1)} %gate.1, bf16[480,3584]{1,0:T(8,128)(2,1)} %up.1), custom_call_target="tpu_custom_call" | custom-call | tf_op jit(solution)/shard_map/pallas_call | solution.py:431
  102.3 1.8 %copy.6 = bf16[1,512,3584]{2,1,0:T(8,128)(2,1)} copy(bf16[1,512,3584]{2,1,0:T(8,128)(2,1)S(1)} %shard_map.46) | data formatting | bytes 7340032

commit v4 on v3

--- a/solution.py
+++ b/solution.py
@@ -20,7 +20,7 @@
 
 def kernel(dims, plan, tok, cot, gate, up, out, ins, grads, toks, tokt, part, got,
            gx, part2, own2, got2, in_sem, own_sem, ty_s, ty_r, tz_s, tz_r, gy_s, gy_r, gp_s, gp_r, x_s, x_r,
-           tx_s, tx_r, gx_s, gx_r, gq_s, gq_r, p2_s, p2_r):
+           tx_s, tx_r, gx_s, gx_r, gq_s, gq_r, p2_s, p2_r, two_in):
     ny, nx, nr, nz, wide, block, chunks, cols = dims
     lead, ahead, own_at, per, lite = plan
     dp, r, z = lax.axis_index("dp"), lax.axis_index("row"), lax.axis_index("col")
@@ -87,10 +87,11 @@
     hops = ([(d, 0) for d in range(reach, 0, -1)] + [(1, d) for d in range(2, nz - 1)])
     relays = max(nz - 3, 0)
 
+    def inside(way, far):
+        return z + far < nz if way > 0 else z >= far
+
     def valid(way, far, back):
-        left = z >= back if way > 0 else z + back < nz
-        right = z + far < nz if way > 0 else z >= far
-        return jnp.logical_and(left, right)
+        return jnp.logical_and(inside(-way, back), inside(way, far))
 
     def relay_sem(w, back, b, oy):
         w = w if nz > 4 else 0
@@ -119,7 +120,10 @@
         def go(way, i):
             far, back = hops[i]
             send = tok_z(b, oy, way, i).start
-            if part == "far":
+            if part in ("one", "two"):
+                if far == (1 if part == "one" else 2):
+                    send()
+            elif part == "far":
                 pl.when(goes_on(way, far, back))(send)
             else:
                 pl.when(jnp.logical_not(goes_on(way, far, back)))(send)
@@ -207,12 +211,20 @@
     for to in peers:
         greet(to)
     met = jnp.int32(len(peers))
-    for far in range(1, reach + 1):
+    for way in (1, -1):
+        there = inside(way, 1)
+        pl.when(there)(functools.partial(greet, at(oz=way + nz)))
+        met = met + jnp.where(there, 1, 0)
+    pl.semaphore_wait(barrier, met)
+
+    def say_on(way):
+        pl.semaphore_signal(two_in.at[max(way, 0)], inc=1, device_id=at(oz=way + nz), device_id_type=MESH)
+    for way in (1, -1):
+        pl.when(jnp.logical_and(inside(-way, 1), inside(way, 1)))(functools.partial(say_on, way))
+
+    def meet():
         for way in (1, -1):
-            there = valid(way, far, 0)
-            pl.when(there)(functools.partial(greet, at(oz=way * far + nz)))
-            met = met + there.astype(jnp.int32)
-    pl.semaphore_wait(barrier, met)
+            pl.when(inside(-way, 2))(lambda w=max(way, 0): pl.semaphore_wait(two_in.at[w], 1))
 
     def tok_out(b):
         for oy in range(1, ny):
@@ -304,12 +316,15 @@
     ended = lambda k: jnp.clip((k - own_at + 1) * per, 0, jnp.minimum(jnp.clip(k - 1, 0, plain), 2 * per))
 
     tok_out(0)
-    own_out(0)
-    rest(0)
+    own_tok(0).wait()
+    send_z(0, 0, "one")
     if lite:
         for i in range(2):
             tok_x(i).start()
-    span(0, lead, feed)
+    span(0, 1, feed)
+    meet()
+    send_z(0, 0, "two")
+    span(1, lead, feed)
 
     def over_x(i):
         gate_grad(plain + i)
@@ -464,6 +479,7 @@
                 dma((more,)),
                 dma((1,)),
                 dma((more,)),
+                pltpu.SemaphoreType.REGULAR((2,)),
             ],
             compiler_params=pltpu.CompilerParams(
                 collective_id=0, has_side_effects=True, vmem_limit_bytes=56 * 1024 * 1024

time: 104 us -> 104 us (level)
  no operation moved by 1% of the time
where the time goes in v4:
time: 104 us
  Pallas kernels  102 us (98%)
  local copies, waits for them, and re-layouts  1.84 us (2%)
    pallas_call x1, Pallas kernels, on_device(): pl.pallas_call(functools.partial(kernel, dims, plan), out_shape=pltpu.VME...  102 us

profile of v4, /device:TPU:0, one launch (start us, length us, event | category | flops | bytes accessed | tf_op | source)
XLA Modules:
  0.0 103.7 jit_solution(14842764858626808457)
XLA Ops:
  0.0 101.9 %shard_map.46 = bf16[1,512,3584]{2,1,0:T(8,128)(2,1)S(1)} custom-call(bf16[240,2048]{1,0:T(8,128)(2,1)} %tok.1, bf16[480,3584]{1,0:T(8,128)(2,1)} %cot.1, bf16[480,3584]{1,0:T(8,128)(2,1)} %gate.1, bf16[480,3584]{1,0:T(8,128)(2,1)} %up.1), custom_call_target="tpu_custom_call" | custom-call | tf_op jit(solution)/shard_map/pallas_call | solution.py:446
  101.9 1.8 %copy.6 = bf16[1,512,3584]{2,1,0:T(8,128)(2,1)} copy(bf16[1,512,3584]{2,1,0:T(8,128)(2,1)S(1)} %shard_map.46) | data formatting | bytes 7340032

commit v5 on v4

--- a/solution.py
+++ b/solution.py
@@ -181,16 +181,16 @@
         return remote(part.at[k, at_rows], got.at[k, at_rows], sent, x_r.at[k], at(ox=b // subs + 1))
 
     def grad_x(i):
-        return remote(grads.at[plain + i, y, r], gx.at[i, x, r], gx_s.at[0], gx_r.at[i], at(ox=1))
+        return remote(grads.at[plain + i, y, r], gx.at[i, x, r], gx_s.at[0], gx_r.at[0], at(ox=1))
 
     def grad_q(i, ox):
         dst = gx.at[i, (x + ox) % nx, r]
         src = dst if ox else grads.at[plain + i, y, r]
-        return remote(src, dst, gq_s.at[0], gq_r.at[i], at(orow=1))
-
-    def got_q(i):
-        ref = gx.at[i, :, (r + 1) % nr]
-        remote(ref, ref, gq_s.at[0], gq_r.at[i], at(orow=1)).wait_recv()
+        return remote(src, dst, gq_s.at[0], gq_r.at[0], at(orow=1))
+
+    def got_q():
+        ref = gx.at[:, :, (r + 1) % nr]
+        remote(ref, ref, gq_s.at[0], gq_r.at[0], at(orow=1)).wait_recv()
 
     def sum_y(i):
         return remote(part2.at[i], got2.at[i], p2_s.at[0], p2_r.at[i], at(oy=1))
@@ -339,16 +339,18 @@
     own_relay(0)
 
     def over_y():
+        ref = gx.at[:, (x + 1) % nx, r]
+        remote(ref, ref, gx_s.at[0], gx_r.at[0], at(ox=1)).wait_recv()
         for i in range(lite):
-            grad_x(i).wait_recv()
             grad_q(i, 1).start()
         take_block(blocks)
         all_z(last, 1)
         toks[last, x] = toks[blocks - 1, y]
         tokt[last * block:, :] = toks[last].reshape(rows, block).T
 
+        got_q()
+
         def sums(i):
-            got_q(i)
             gx[i, x, r] = grads[plain + i, y, r]
             both = jnp.dot(tokt[blocks * block:, :], gx[i].reshape(rows, cols), preferred_element_type=jnp.float32)
             part2[i] = both[:block].astype(part2.dtype)
@@ -440,7 +442,7 @@
         more = max(lite, 1)
         relays = (2 if nz > 4 else 1) * max(nz - 3, 0) * every * ny
         dims = (ny, nx, nr, nz, wide, block, chunks, cols)
-        plan = (3, min(5, chunks), max(chunks - 4, 0), 3, lite)
+        plan = (2, min(5, chunks), max(chunks - 4, 0), 3, lite)
         dma = pltpu.SemaphoreType.DMA
         dt = tokens.dtype
         return pl.pallas_call(
@@ -474,9 +476,9 @@
                 dma((1,)),
                 dma((2,)),
                 dma((1,)),
-                dma((more,)),
-                dma((1,)),
-                dma((more,)),
+                dma((1,)),
+                dma((1,)),
+                dma((1,)),
                 dma((1,)),
                 dma((more,)),
                 pltpu.SemaphoreType.REGULAR((2,)),

time: 104 us -> 104 us (level)
  no operation moved by 1% of the time
where the time goes in v5:
time: 104 us
  Pallas kernels  102 us (98%)
  local copies, waits for them, and re-layouts  1.84 us (2%)
    pallas_call x1, Pallas kernels, on_device(): pl.pallas_call(functools.partial(kernel, dims, plan), out_shape=pltpu.VME...  102 us

profile of v5, /device:TPU:0, one launch (start us, length us, event | category | flops | bytes accessed | tf_op | source)
XLA Modules:
  0.0 104.0 jit_solution(171856544147837190)
XLA Ops:
  0.0 102.1 %shard_map.46 = bf16[1,512,3584]{2,1,0:T(8,128)(2,1)S(1)} custom-call(bf16[240,2048]{1,0:T(8,128)(2,1)} %tok.1, bf16[480,3584]{1,0:T(8,128)(2,1)} %cot.1, bf16[480,3584]{1,0:T(8,128)(2,1)} %gate.1, bf16[480,3584]{1,0:T(8,128)(2,1)} %up.1), custom_call_target="tpu_custom_call" | custom-call | tf_op jit(solution)/shard_map/pallas_call | solution.py:448
  102.1 1.8 %copy.6 = bf16[1,512,3584]{2,1,0:T(8,128)(2,1)} copy(bf16[1,512,3584]{2,1,0:T(8,128)(2,1)S(1)} %shard_map.46) | data formatting | bytes 7340032
